TPU v7x, 128 devices: a whole 4x4x4 slice. The times are simulated.
128 devices in a mesh: grp: 4 (over z), kv: 16 (over x, y), tp: 2 (over core).
Axes of the slice: x: 4, y: 4, z: 4, core: 2. Of those that a mesh axis runs over, the one named last changes fastest.
Arguments:
- hidden_states: bfloat16 [512, 4096], P('grp', 'kv'), may hold values from -6 to 6
- attn_gain: float32 [4096], P('kv'), may hold values from 0.25 to 1.75
- mlp_gain: float32 [4096], replicated, may hold values from 0.25 to 1.75
- w_query: bfloat16 [4096, 4096], P('kv', 'tp'), may hold values from -0.09375 to 0.09375
- w_out: bfloat16 [32, 128, 4096], P('tp', 'kv'), may hold values from -1 to 1
- w_gate: bfloat16 [4096, 14336], P(None, ('kv', 'tp')), may hold values from -0.09375 to 0.09375
- w_up: bfloat16 [4096, 14336], P(None, ('kv', 'tp')), may hold values from -0.09375 to 0.09375
- w_down: bfloat16 [14336, 4096], P(('kv', 'tp')), may hold values from -0.046875 to 0.046875
- kv_pool: bfloat16 [1024, 2, 128, 1024], P(('grp', 'kv'), None, None, 'tp'), may hold values from -110 to 110
- resident_cache: bfloat16 [4, 128, 2, 128, 1024], P('grp', 'kv', None, None, 'tp'), may hold values from -110 to 110
- resident_slot: int32 [4, 128], P('grp', 'kv'), may hold values from 0 to 127
- resident_len: int32 [4, 128], P('grp', 'kv'), may hold values from 1 to 128
- new_owner: int32 [4, 256], replicated, may hold values from 0 to 63, as said below
- new_local: int32 [4, 256], replicated, may hold values from 0 to 15
- new_slot: int32 [4, 256], P('grp', 'kv'), may hold values from 0 to 127
- new_len: int32 [4, 256], P('grp', 'kv'), may hold values from 1 to 128
- token_kv: bfloat16 [512, 2, 1024], P('grp', None, 'tp'), may hold values from -6 to 6
Outputs:
- mixed: bfloat16 [512, 4096], P(('grp', 'kv', 'tp'))
- new_cache: bfloat16 [4, 256, 2, 128, 1024], P('grp', 'kv', None, None, 'tp')
Inputs may be any that keep to these rules, and one draw needn't show every extreme that they name: New page c of group g is kept by the device of kv index c // 16 of group g and comes from the device whose index along grp+kv is new_owner[g, c]; every decode device receives exactly 4 new pages from the owners of each grp index; no owner sends more than 1 pages to the devices of one kv index over all groups, so at most 1 to one device; every owner sends each of its 16 pages exactly once.
All inputs are finite; a program needn't handle non-finite values.
Results may differ from a plain program's by a relative error of at most 0.018.
Values may be sent and summed in bfloat16 or wider, within the bound.
A program may use at most 128 MiB of HBM per device.

v0:
```python
import jax
import jax.numpy as jnp
from jax import lax
from jax.sharding import Mesh
from jax.sharding import PartitionSpec as P

D = 4096
HEADS = 32
KV_HEADS = 8
HEAD_DIM = 128
NPR = 4
KV = ("kv_0", "kv_1")
KV_TP = ("kv_0", "kv_1", "tp")
GRP_KV = ("grp", "kv_0", "kv_1")
GRP_KV_TP = ("grp", "kv_0", "kv_1", "tp")
neg_fill = -1e30
norm_eps = 1e-05


def combined_by_axis(shard, axes, combine):
    for axis in axes:
        pieces = jax.tree.map(lambda part: lax.all_gather(part, axis), shard)
        shard = jax.tree.map(lambda part: part[0], pieces)
        for k in range(1, lax.axis_size(axis)):
            shard = combine(shard, jax.tree.map(lambda part: part[k], pieces))
    return shard


def split_up(shard, dim, peers):
    before, after = (shard.shape[:dim], shard.shape[dim + 1 :])
    return jnp.moveaxis(shard.reshape(*before, peers, -1, *after), dim, 0)


def summed_on_arrival(shard, axis, dim):
    tiles = split_up(shard, dim, lax.axis_size(axis))
    arrived = lax.all_to_all(tiles, axis, split_axis=0, concat_axis=0, tiled=True)
    return arrived.astype(jnp.float32).sum(axis=0)


def combine(earlier, later):
    top_a, sum_a, acc_a = earlier
    top_b, sum_b, acc_b = later
    top = jnp.maximum(top_a, top_b)
    fade_a = jnp.exp(top_a - top)
    fade_b = jnp.exp(top_b - top)
    return (
        top,
        sum_a * fade_a + sum_b * fade_b,
        acc_a * fade_a[..., None] + acc_b * fade_b[..., None],
    )


def nth_match(table, wanted, places):
    matched = (table == wanted).astype(jnp.int32)
    ranking = jnp.cumsum(matched, axis=1) - 1
    return (matched[:, None, :] == 1) & (ranking[:, None, :] == places[None, :, None])


def move_pages(kv_pool, new_owner, new_local):
    groups = lax.axis_size("grp")
    ranks = lax.axis_size(KV)
    per_dev = new_owner.shape[1] // ranks
    cap = groups * NPR // ranks
    grp_rank = lax.axis_index("grp")
    kv_rank = lax.axis_index(KV)
    owners = new_owner.reshape(groups * ranks, per_dev)
    myself = grp_rank * ranks + kv_rank
    places = jnp.arange(cap, dtype=jnp.int32)
    mine = lax.dynamic_index_in_dim(owners, myself, 0, keepdims=False)
    order = jnp.arange(per_dev, dtype=jnp.int32)
    by_col = (
        new_owner.reshape(groups, ranks, per_dev)
        .transpose(1, 0, 2)
        .reshape(ranks, groups * per_dev)
    )
    local_col = (
        new_local.reshape(groups, ranks, per_dev)
        .transpose(1, 0, 2)
        .reshape(ranks, groups * per_dev)
    )
    select = nth_match(by_col, myself, places)
    picked = jnp.sum(jnp.where(select, local_col[:, None, :], 0), axis=2)
    outgoing = jnp.take(kv_pool, picked.reshape(-1), axis=0)
    received = lax.all_to_all(outgoing, KV, split_axis=0, concat_axis=0, tiled=True)
    row_here = lax.dynamic_index_in_dim(by_col, kv_rank, 0, keepdims=False)
    sources = grp_rank * ranks + jnp.arange(ranks, dtype=jnp.int32)
    hits = nth_match(
        jnp.broadcast_to(row_here[None, :], (ranks, row_here.shape[0])), sources[:, None], places
    )
    spots = jnp.arange(row_here.shape[0], dtype=jnp.int32)
    where_f = jnp.sum(jnp.where(hits, spots[None, None, :], 0), axis=2).reshape(-1)
    dest_grp = where_f // per_dev
    dest_pos = where_f % per_dev
    same = (dest_grp[:, None] == dest_grp[None, :]) & (dest_pos[:, None] < dest_pos[None, :])
    rank_in = jnp.sum(same.astype(jnp.int32), axis=0)
    target = dest_grp * NPR + rank_in
    items = jnp.arange(target.shape[0], dtype=jnp.int32)
    inverse = jnp.sum(jnp.where(target[None, :] == items[:, None], items[None, :], 0), axis=1)
    sorted_pages = jnp.take(received, inverse, axis=0)
    arrived = lax.all_to_all(sorted_pages, "grp", split_axis=0, concat_axis=0, tiled=True)
    src_grp = mine // ranks
    earlier = (src_grp[:, None] == src_grp[None, :]) & (order[:, None] < order[None, :])
    before = jnp.sum(earlier.astype(jnp.int32), axis=0)
    return jnp.take(arrived, src_grp * NPR + before, axis=0)


def local_partials(query, resident, arrived, res_slot, res_len, arr_slot, arr_len, token_kv, first):
    pages = jnp.concatenate([resident, arrived], axis=0)
    owner_slot = jnp.concatenate([res_slot, arr_slot])
    filled = jnp.concatenate([res_len, arr_len])
    count = pages.shape[0]
    tokens = pages.shape[2]
    kv_here = pages.shape[3] // HEAD_DIM
    slots = query.shape[0]
    ratio = HEADS // KV_HEADS
    keys = pages[:, 0].astype(jnp.float32).reshape(count, tokens, kv_here, HEAD_DIM)
    values = pages[:, 1].astype(jnp.float32).reshape(count, tokens, kv_here, HEAD_DIM)
    grouped = query.reshape(slots, kv_here, ratio, HEAD_DIM)
    picked = jnp.take(grouped, owner_slot, axis=0)
    scores = jnp.einsum("ikgd,itkd->ikgt", picked, keys, precision=lax.Precision.HIGHEST)
    usable = (jnp.arange(tokens, dtype=jnp.int32)[None, :] < filled[:, None])[:, None, None, :]
    scores = jnp.where(usable, scores, neg_fill)
    page_top = jnp.max(scores, axis=3)
    member = owner_slot[None, :] == jnp.arange(slots, dtype=jnp.int32)[:, None]
    slot_top = jnp.max(jnp.where(member[:, :, None, None], page_top[None], neg_fill), axis=1)
    own_keys = token_kv[:, 0].astype(jnp.float32).reshape(slots, kv_here, HEAD_DIM)
    own_values = token_kv[:, 1].astype(jnp.float32).reshape(slots, kv_here, HEAD_DIM)
    own_score = jnp.einsum("skgd,skd->skg", grouped, own_keys, precision=lax.Precision.HIGHEST)
    own_score = jnp.where(first, own_score, neg_fill)
    slot_top = jnp.maximum(slot_top, own_score)
    reach = jnp.take(slot_top, owner_slot, axis=0)
    weights = jnp.where(usable, jnp.exp(scores - reach[..., None]), 0.0)
    page_sum = jnp.sum(weights, axis=3)
    page_acc = jnp.einsum("ikgt,itkd->ikgd", weights, values, precision=lax.Precision.HIGHEST)
    own_weight = jnp.where(first, jnp.exp(own_score - slot_top), 0.0)
    member_f = member.astype(jnp.float32)
    total = jnp.dot(member_f, page_sum.reshape(count, -1), precision=lax.Precision.HIGHEST)
    total = total + own_weight.reshape(slots, -1)
    weighted = jnp.dot(member_f, page_acc.reshape(count, -1), precision=lax.Precision.HIGHEST)
    weighted = (
        weighted.reshape(slots, kv_here, ratio, HEAD_DIM)
        + own_weight[..., None] * own_values[:, :, None, :]
    )
    return (slot_top.reshape(slots, -1), total, weighted.reshape(slots, kv_here * ratio, HEAD_DIM))


def per_device(
    hidden_states,
    attn_gain,
    mlp_gain,
    w_query,
    w_out,
    w_gate,
    w_up,
    w_down,
    kv_pool,
    resident_cache,
    resident_slot,
    resident_len,
    new_owner,
    new_local,
    new_slot,
    new_len,
    token_kv,
):
    ranks = lax.axis_size(KV)
    pairs = lax.axis_size("tp")
    kv_rank = lax.axis_index(KV)
    tp_rank = lax.axis_index("tp")
    features = hidden_states.astype(jnp.float32)
    partial_query = jnp.dot(
        (features * attn_gain).astype(jnp.bfloat16), w_query, preferred_element_type=jnp.float32
    )
    squares = jnp.sum(features * features, axis=1)
    partial_query, squares = lax.psum((partial_query, squares), KV)
    attn_scale = lax.rsqrt(squares / D + norm_eps)
    query = partial_query * attn_scale[:, None] * HEAD_DIM ** (-0.5)
    new_pages = move_pages(kv_pool, new_owner, new_local)
    top, total, weighted = local_partials(
        query,
        resident_cache[0],
        new_pages,
        resident_slot[0],
        resident_len[0],
        new_slot[0],
        new_len[0],
        token_kv,
        kv_rank == 0,
    )
    top, total, weighted = combined_by_axis((top, total, weighted), KV, combine)
    attn = (weighted / total[..., None]).astype(jnp.bfloat16)
    slots = attn.shape[0]
    heads_here = attn.shape[1]
    span = HEAD_DIM // ranks
    piece = lax.dynamic_slice_in_dim(attn, kv_rank * span, span, 2)
    branch = jnp.dot(
        piece.reshape(slots, heads_here * span),
        w_out.reshape(heads_here * span, w_out.shape[2]),
        preferred_element_type=jnp.float32,
    )
    width_here = hidden_states.shape[1]
    laid = branch.reshape(slots, ranks, width_here)
    spot = (jnp.arange(ranks, dtype=jnp.int32) == kv_rank) & (tp_rank == 0)
    laid = laid + jnp.where(spot[None, :, None], features[:, None, :], 0.0)
    resid = lax.psum(laid.reshape(slots, ranks * width_here).astype(jnp.bfloat16), KV_TP)
    resid_f = resid.astype(jnp.float32)
    mlp_scale = lax.rsqrt(jnp.sum(resid_f * resid_f, axis=1) / D + norm_eps)
    normed_mlp = (resid_f * mlp_gain).astype(jnp.bfloat16)
    gate = jnp.dot(normed_mlp, w_gate, preferred_element_type=jnp.float32) * mlp_scale[:, None]
    upward = jnp.dot(normed_mlp, w_up, preferred_element_type=jnp.float32) * mlp_scale[:, None]
    hidden_units = (jax.nn.silu(gate) * upward).astype(jnp.bfloat16)
    row_count = slots // (ranks * pairs)
    down = summed_on_arrival(
        jnp.dot(hidden_units, w_down, preferred_element_type=jnp.float32).astype(jnp.bfloat16),
        KV_TP,
        0,
    )
    row_start = (kv_rank * pairs + tp_rank) * row_count
    kept = lax.dynamic_slice_in_dim(resid_f, row_start, row_count, 0)
    mixed = (kept + down).astype(jnp.bfloat16)
    return (mixed, new_pages[None])


def solution(mesh):
    finer = Mesh(
        mesh.devices.reshape(mesh.shape["grp"], 4, 4, mesh.shape["tp"]),
        ("grp", "kv_0", "kv_1", "tp"),
    )
    return jax.shard_map(
        per_device,
        mesh=finer,
        in_specs=(
            P("grp", KV),
            P(KV),
            P(),
            P(KV, "tp"),
            P("tp", KV, None),
            P(None, KV_TP),
            P(None, KV_TP),
            P(KV_TP, None),
            P(GRP_KV, None, None, "tp"),
            P("grp", KV, None, None, "tp"),
            P("grp", KV),
            P("grp", KV),
            P(),
            P(),
            P("grp", KV),
            P("grp", KV),
            P("grp", None, "tp"),
        ),
        out_specs=(P(GRP_KV_TP, None), P("grp", KV, None, None, "tp")),
        check_vma=False,
    )
```

profile of v0, /device:TPU:1, one launch (start us, length us, event | category | flops | bytes accessed | tf_op | source)
XLA Modules:
  0.0 507.7 jit_solution(3619202428460434715)
XLA Ops:
  10.4 5.0 gather_fusion.2
  15.5 4.7 broadcast_select_fusion.2
  20.1 7.6 %all-to-all-start = ((bf16[16,2,128,512]{3,2,1,0:T(8,128)(2,1)}), bf16[16,2,128,512]{3,2,1,0:T(8,128)(2,1)}, u32[]{:S(2)}, u32[]{:S(2)}) async-start(bf16[16,2,128,512]{3,2,1,0:T(8,128)(2,1)} %broadcast_select_fusion.2), calls=%async_computation | async-start | bytes 8388608 | tf_op jit(solution)/shard_map/all_to_all | solution.py:84
  28.5 59.5 %all-to-all-done = bf16[16,2,128,512]{3,2,1,0:T(8,128)(2,1)} async-done(((bf16[16,2,128,512]{3,2,1,0:T(8,128)(2,1)}), bf16[16,2,128,512]{3,2,1,0:T(8,128)(2,1)}, u32[]{:S(2)}, u32[]{:S(2)}) %all-to-all-start) | async-done | bytes 4194336 | tf_op jit(solution)/shard_map/all_to_all | solution.py:84
  88.1 5.0 gather_fusion.3
  93.1 4.7 broadcast_select_fusion.1
  97.8 5.2 %all-to-all-start.1 = ((bf16[16,2,128,512]{3,2,1,0:T(8,128)(2,1)}), bf16[16,2,128,512]{3,2,1,0:T(8,128)(2,1)}, u32[]{:S(2)}, u32[]{:S(2)}) async-start(bf16[16,2,128,512]{3,2,1,0:T(8,128)(2,1)} %broadcast_select_fusion.1), calls=%async_computation.1 | async-start | bytes 8388608 | tf_op jit(solution)/shard_map/all_to_all | solution.py:100
  105.6 33.9 %psum.22 = f32[128]{0:T(128)S(1)} all-reduce(f32[128]{0:T(128)S(1)} %multiply_reduce_fusion.1), channel_id=1, replica_groups=mesh['grp'=4,'kv_0'=4,'kv_1'=4,'tp'=2] {'kv_0','kv_1'}, use_global_device_ids=true, to_apply=%region_2.0 | all-reduce | flops 128 | bytes 1024 | tf_op jit(solution)/shard_map/psum | solution.py:175
  139.8 61.1 %all-reduce.3.cloned.1.call-done = f32[128,2048]{1,0:T(8,128)} async-done(((f32[128,2048]{1,0:T(8,128)}), f32[128,2048]{1,0:T(8,128)}) %all-reduce.3.cloned.1.call-update) | async-done | bytes 1048592 | tf_op jit(solution)/shard_map/psum | solution.py:175
  203.7 1.8 fusion.81
  205.5 5.0 gather_fusion.4
  210.6 2.8 broadcast_select_fusion
  213.4 2.9 pad_maximum_fusion
  216.3 4.7 copy.150
  221.0 4.6 fusion.80
  227.0 4.7 copy.155
  231.7 6.9 %fusion.17 = f32[24,4,4,128]{3,2,1,0:T(4,128)S(1)} fusion(bf16[24,128,4,128]{1,3,2,0:T(8,128)(2,1)} %bitcast.217, f32[24,4,4,128]{3,2,1,0:T(4,128)S(1)} %get-tuple-element.40, f32[24,4,4]{2,1,0:T(4,128)S(1)} %broadcast_select_fusion.3, pred[24,128]{1,0:T(8,128)(4,1)S(1)} %iota_compare_fusion), kind=kOutput, calls=%fused_computation.52 | convolution fusion | flops 75595776 | bytes 3543552 | tf_op jit(solution)/shard_map/ikgt,itkd->ikgd/dot_general | solution.py:134
  241.4 9.3 %all_gather.25 = f32[4,128,16]{1,2,0:T(8,128)S(1)} all-gather(f32[1,128,16]{1,2,0:T(8,128)S(1)} %bitcast.229), channel_id=1, replica_groups=mesh['grp'=4,'kv_0'=4,'kv_1'=4,'tp'=2] {'kv_0'}, dimensions={0}, use_global_device_ids=true | all-gather | bytes 40960 | tf_op jit(solution)/shard_map/all_gather | solution.py:22
  251.3 38.9 %all-gather.4.cloned.1.call-done = f32[4,128,16,128]{3,2,1,0:T(8,128)} async-done(((f32[1,128,16,128]{3,2,1,0:T(8,128)}), f32[4,128,16,128]{3,2,1,0:T(8,128)}) %all-gather.4.cloned.1.call-update) | async-done | bytes 4194320 | tf_op jit(solution)/shard_map/all_gather | solution.py:22
  290.2 4.8 fusion.3
  297.1 9.0 %all-gather = f32[512,16]{0,1:T(8,128)S(1)} all-gather(f32[128,16]{0,1:T(8,128)S(1)} %convolution_add_fusion.1), channel_id=2, replica_groups=mesh['grp'=4,'kv_0'=4,'kv_1'=4,'tp'=2] {'kv_0'}, dimensions={0}, use_global_device_ids=true | all-gather | bytes 40960 | tf_op jit(solution)/shard_map/all_gather | solution.py:22
  306.2 10.8 %all_gather.27 = f32[4,128,16]{1,2,0:T(8,128)S(1)} all-gather(f32[1,128,16]{1,2,0:T(8,128)S(1)} %get-tuple-element.15), channel_id=1, replica_groups=mesh['grp'=4,'kv_0'=4,'kv_1'=4,'tp'=2] {'kv_1'}, dimensions={0}, use_global_device_ids=true | all-gather | bytes 40960 | tf_op jit(solution)/shard_map/all_gather | solution.py:22
  317.0 10.6 %all_gather.30 = f32[4,128,16]{1,2,0:T(8,128)S(1)} all-gather(f32[1,128,16]{1,2,0:T(8,128)S(1)} %get-tuple-element.14), channel_id=1, replica_groups=mesh['grp'=4,'kv_0'=4,'kv_1'=4,'tp'=2] {'kv_1'}, dimensions={0}, use_global_device_ids=true | all-gather | bytes 40960 | tf_op jit(solution)/shard_map/all_gather | solution.py:22
  327.6 16.7 %all-gather.6.cloned.1.call-done = f32[4,128,16,128]{3,2,1,0:T(8,128)} async-done(((f32[1,128,16,128]{3,2,1,0:T(8,128)}), f32[4,128,16,128]{3,2,1,0:T(8,128)}) %all-gather.6.cloned.1.call-update) | async-done | bytes 4194320 | tf_op jit(solution)/shard_map/all_gather | solution.py:22
  344.3 3.9 fusion.78
  350.2 2.6 copy.188
  358.2 105.7 %all-reduce.5.cloned.1.call-done = bf16[128,4096]{1,0:T(8,128)(2,1)} async-done(((bf16[128,4096]{1,0:T(8,128)(2,1)}), bf16[128,4096]{1,0:T(8,128)(2,1)}) %all-reduce.5.cloned.1.call-update) | async-done | bytes 1048592 | tf_op jit(solution)/shard_map/psum | solution.py:205
  465.5 3.5 convolution_multiply_fusion.1
  469.0 6.0 %convolution_convert_fusion = bf16[128,4096]{1,0:T(8,128)(2,1)S(1)} fusion(bf16[448,4096]{1,0:T(8,128)(2,1)} %param.26, bf16[4096,448]{0,1:T(8,128)(2,1)} %param.25, f32[4096]{0:T(1024)S(1)} %copy-done.7, bf16[128,4096]{1,0:T(8,128)(2,1)S(1)} %copy-done.2, f32[128,448]{0,1:T(8,128)S(1)} %convolution_multiply_fusion.1, f32[128]{0:T(128)S(1)} %add_rsqrt_fusion), kind=kOutput, calls=%fused_computation.7 | convolution fusion | flops 942022656 | bytes 9683456 | tf_op jit(solution)/shard_map/dot_general | solution.py:214
  476.3 6.1 %all-to-all-start.2 = ((bf16[32,4,4096]{2,1,0:T(4,128)(2,1)}), bf16[32,4,4096]{2,1,0:T(4,128)(2,1)S(1)}, u32[]{:S(2)}, u32[]{:S(2)}) async-start(bf16[32,4,4096]{2,1,0:T(4,128)(2,1)} %reshape.671), calls=%async_computation.2 | async-start | bytes 2097152 | tf_op jit(solution)/shard_map/all_to_all | solution.py:36
  482.3 4.8 fusion.92
  488.7 10.6 %all-to-all-done.2 = bf16[32,4,4096]{2,1,0:T(4,128)(2,1)S(1)} async-done(((bf16[32,4,4096]{2,1,0:T(4,128)(2,1)}), bf16[32,4,4096]{2,1,0:T(4,128)(2,1)S(1)}, u32[]{:S(2)}, u32[]{:S(2)}) %all-to-all-start.2) | async-done | bytes 1048608 | tf_op jit(solution)/shard_map/all_to_all | solution.py:36
  (121 shorter events, 30.3 us)
Async XLA Ops:
  7.2 95.8 %copy-start = (bf16[256,2048]{1,0:T(8,128)(2,1)S(1)}, bf16[256,2048]{1,0:T(8,128)(2,1)}, u32[]{:S(2)}) copy-start(bf16[256,2048]{1,0:T(8,128)(2,1)} %param.22) | copy-start | bytes 3145732
  20.1 68.0 %all-to-all-start = ((bf16[16,2,128,512]{3,2,1,0:T(8,128)(2,1)}), bf16[16,2,128,512]{3,2,1,0:T(8,128)(2,1)}, u32[]{:S(2)}, u32[]{:S(2)}) async-start(bf16[16,2,128,512]{3,2,1,0:T(8,128)(2,1)} %broadcast_select_fusion.2), calls=%async_computation | async-start | bytes 8388608 | tf_op jit(solution)/shard_map/all_to_all | solution.py:84
  97.8 5.3 %copy-start.6 = (bf16[128,256]{1,0:T(8,128)(2,1)S(1)}, bf16[128,256]{1,0:T(8,128)(2,1)}, u32[]{:S(2)}) copy-start(bf16[128,256]{1,0:T(8,128)(2,1)} %param.19) | copy-start | bytes 196612
  97.8 5.3 %copy-start.8 = (f32[256]{0:T(256)S(1)}, f32[256]{0:T(256)}, u32[]{:S(2)}) copy-start(f32[256]{0:T(256)} %param.20) | copy-start | bytes 3076
  97.8 6.7 %copy-start.9 = (s32[1,16]{1,0:T(1,128)S(1)}, s32[1,16]{1,0:T(1,128)}, u32[]{:S(2)}) copy-start(s32[1,16]{1,0:T(1,128)} %param.33) | copy-start | bytes 196
  97.8 6.7 %copy-start.10 = (s32[1,8]{1,0:T(1,128)S(1)}, s32[1,8]{1,0:T(1,128)}, u32[]{:S(2)}) copy-start(s32[1,8]{1,0:T(1,128)} %param.29) | copy-start | bytes 100
  97.8 7.0 %copy-start.5 = (bf16[128,2,512]{2,1,0:T(2,128)(2,1)S(1)}, bf16[128,2,512]{2,1,0:T(2,128)(2,1)}, u32[]{:S(2)}) copy-start(bf16[128,2,512]{2,1,0:T(2,128)(2,1)} %param.35) | copy-start | bytes 786436
  97.8 107.8 %all-to-all-start.1 = ((bf16[16,2,128,512]{3,2,1,0:T(8,128)(2,1)}), bf16[16,2,128,512]{3,2,1,0:T(8,128)(2,1)}, u32[]{:S(2)}, u32[]{:S(2)}) async-start(bf16[16,2,128,512]{3,2,1,0:T(8,128)(2,1)} %broadcast_select_fusion.1), calls=%async_computation.1 | async-start | bytes 8388608 | tf_op jit(solution)/shard_map/all_to_all | solution.py:100
  103.0 2.2 copy-start.11
  103.0 2.2 copy-start.12
  103.0 98.0 %all-reduce.3.cloned.1.call-start = ((), (), s32[]{:S(2)}) async-start(), calls=%async_computation.3 | async-start | bytes 2097152 | tf_op jit(solution)/shard_map/psum | solution.py:175
  104.4 185.8 %all-gather.4.cloned.1.call-start = ((), (), s32[]{:S(2)}) async-start(), calls=%async_computation.4 | async-start | bytes 5242880 | tf_op jit(solution)/shard_map/all_gather | solution.py:22
  210.6 2.9 copy-start.3
  241.2 103.0 %all-gather.6.cloned.1.call-start = ((), (), s32[]{:S(2)}) async-start(), calls=%async_computation.5 | async-start | bytes 5242880 | tf_op jit(solution)/shard_map/all_gather | solution.py:22
  250.7 44.4 %copy-start.4 = (bf16[16,8,4096]{2,1,0:T(8,128)(2,1)S(1)}, bf16[16,8,4096]{2,1,0:T(8,128)(2,1)}, u32[]{:S(2)}) copy-start(bf16[16,8,4096]{2,1,0:T(8,128)(2,1)} %param.23) | copy-start | bytes 3145732
  295.0 168.9 %all-reduce.5.cloned.1.call-start = ((), (), s32[]{:S(2)}) async-start(), calls=%async_computation.6 | async-start | bytes 2097152 | tf_op jit(solution)/shard_map/psum | solution.py:205
  356.2 109.3 %copy-start.7 = (f32[4096]{0:T(1024)S(1)}, f32[4096]{0:T(1024)}, u32[]{:S(2)}) copy-start(f32[4096]{0:T(1024)} %param.21) | copy-start | bytes 49156
  463.9 5.1 %copy-start.2 = (bf16[128,4096]{1,0:T(8,128)(2,1)S(1)}, bf16[128,4096]{1,0:T(8,128)(2,1)}, u32[]{:S(2)}) copy-start(bf16[128,4096]{1,0:T(8,128)(2,1)} %all-reduce.5.cloned.1.call-done) | copy-start | bytes 3145732
  476.3 23.0 %all-to-all-start.2 = ((bf16[32,4,4096]{2,1,0:T(4,128)(2,1)}), bf16[32,4,4096]{2,1,0:T(4,128)(2,1)S(1)}, u32[]{:S(2)}, u32[]{:S(2)}) async-start(bf16[32,4,4096]{2,1,0:T(4,128)(2,1)} %reshape.671), calls=%async_computation.2 | async-start | bytes 2097152 | tf_op jit(solution)/shard_map/all_to_all | solution.py:36
  482.3 18.9 %copy-start.1 = (bf16[256,2048]{1,0:T(8,128)(2,1)S(1)}, bf16[256,2048]{1,0:T(8,128)(2,1)}, u32[]{:S(2)}) copy-start(bf16[256,2048]{1,0:T(8,128)(2,1)} %param.22) | copy-start | bytes 3145732
Sparse Core Ops, SparseCore 0:
  107.0 93.8 all-reduce.2
  241.4 48.7 all-gather.3
  295.1 49.0 all-gather.5
  358.4 105.4 all-reduce.4
where the time goes:
time: 509 us; the launch traced here: 508 us
  waiting for transfers between devices  292 us (57%)
  blocking collectives  73.6 us (14%)
  local copies, waits for them, and re-layouts  47 us (9%)
  other arithmetic  34.5 us (7%)
  matrix products  26.8 us (5%)
  starting transfers between devices  19 us (4%)
  between operations  14.2 us (3%)
    psum x1, waiting for transfers between devices, per_device(): lax.psum(laid.reshape(slots, ranks * width_here).astype(jnp.bfloat16), KV...  106 us
    psum x1, waiting for transfers between devices, per_device(): partial_query, squares = lax.psum((partial_query, squares), KV)  61.1 us
    all_to_all x1, waiting for transfers between devices, move_pages(): lax.all_to_all(outgoing, KV, split_axis=0, concat_axis=0, tiled=True)  59.5 us
    all_gather x2, waiting for transfers between devices, combined_by_axis(): pieces = jax.tree.map(lambda part: lax.all_gather(part, axis), shard)  55.5 us
    all_gather x4, blocking collectives, combined_by_axis(): pieces = jax.tree.map(lambda part: lax.all_gather(part, axis), shard)  39.7 us
    psum x1, blocking collectives, per_device(): partial_query, squares = lax.psum((partial_query, squares), KV)  33.9 us
    all_to_all x1, waiting for transfers between devices, summed_on_arrival(): lax.all_to_all(tiles, axis, split_axis=0, concat_axis=0, tiled=True)  10.6 us
  transfers between devices with their start and end apart: 7, of which 6 were waited for; matrix products, arithmetic and copies ran while one was open for 3% of the time, Pallas kernels for 0%

commit v1 on v0

--- a/solution.py
+++ b/solution.py
@@ -202,7 +202,9 @@
     laid = branch.reshape(slots, ranks, width_here)
     spot = (jnp.arange(ranks, dtype=jnp.int32) == kv_rank) & (tp_rank == 0)
     laid = laid + jnp.where(spot[None, :, None], features[:, None, :], 0.0)
-    resid = lax.psum(laid.reshape(slots, ranks * width_here).astype(jnp.bfloat16), KV_TP)
+    resid = jnp.sum(
+        lax.all_gather(laid.reshape(slots, ranks * width_here).astype(jnp.bfloat16), KV_TP), axis=0
+    )
     resid_f = resid.astype(jnp.float32)
     mlp_scale = lax.rsqrt(jnp.sum(resid_f * resid_f, axis=1) / D + norm_eps)
     normed_mlp = (resid_f * mlp_gain).astype(jnp.bfloat16)

time: 509 us -> 535 us (1.051)
  other arithmetic: 34.5 us -> 46.3 us
  waiting for transfers between devices: 292 us -> 303 us
    all_gather x0 -> x1, waiting for transfers between devices: none -> 115 us  [per_device(): lax.all_gather(laid.reshape(slots, ranks * width_here).astype(jnp.bfloat1...]
    psum x1 -> x0, waiting for transfers between devices: 106 us -> none  [per_device(): lax.psum(laid.reshape(slots, ranks * width_here).astype(jnp.bfloat16), KV...]
    reduce_sum x0 -> x1, other arithmetic: none -> 11.4 us  [per_device(): jnp.sum(lax.all_gather(laid.reshape(slots, ranks * width_here).astype(jnp...]
where the time goes in v1:
time: 535 us; the launch traced here: 534 us
  waiting for transfers between devices  303 us (57%)
  blocking collectives  73.6 us (14%)
  local copies, waits for them, and re-layouts  51.9 us (10%)
  other arithmetic  46.3 us (9%)
  matrix products  26.7 us (5%)
  starting transfers between devices  18.2 us (3%)
  between operations  14.2 us (3%)
    all_gather x1, waiting for transfers between devices, per_device(): lax.all_gather(laid.reshape(slots, ranks * width_here).astype(jnp.bfloat1...  115 us
    psum x1, waiting for transfers between devices, per_device(): partial_query, squares = lax.psum((partial_query, squares), KV)  61.2 us
    all_to_all x1, waiting for transfers between devices, move_pages(): lax.all_to_all(outgoing, KV, split_axis=0, concat_axis=0, tiled=True)  59.5 us
    all_gather x2, waiting for transfers between devices, combined_by_axis(): pieces = jax.tree.map(lambda part: lax.all_gather(part, axis), shard)  55.5 us
    all_gather x4, blocking collectives, combined_by_axis(): pieces = jax.tree.map(lambda part: lax.all_gather(part, axis), shard)  39.7 us
    psum x1, blocking collectives, per_device(): partial_query, squares = lax.psum((partial_query, squares), KV)  33.8 us
    all_to_all x1, waiting for transfers between devices, summed_on_arrival(): lax.all_to_all(tiles, axis, split_axis=0, concat_axis=0, tiled=True)  12.1 us
    reduce_sum x1, other arithmetic, per_device(): jnp.sum(lax.all_gather(laid.reshape(slots, ranks * width_here).astype(jnp...  11.4 us
  transfers between devices with their start and end apart: 7, of which 6 were waited for; matrix products, arithmetic and copies ran while one was open for 3% of the time, Pallas kernels for 0%

profile of v1, /device:TPU:1, one launch (start us, length us, event | category | flops | bytes accessed | tf_op | source)
XLA Modules:
  0.0 533.9 jit_solution(9298590138253661782)
XLA Ops:
  10.4 5.0 gather_fusion.2
  15.5 4.7 broadcast_select_fusion.2
  20.1 7.6 %all-to-all-start = ((bf16[16,2,128,512]{3,2,1,0:T(8,128)(2,1)}), bf16[16,2,128,512]{3,2,1,0:T(8,128)(2,1)}, u32[]{:S(2)}, u32[]{:S(2)}) async-start(bf16[16,2,128,512]{3,2,1,0:T(8,128)(2,1)} %broadcast_select_fusion.2), calls=%async_computation | async-start | bytes 8388608 | tf_op jit(solution)/shard_map/all_to_all | solution.py:84
  28.5 59.5 %all-to-all-done = bf16[16,2,128,512]{3,2,1,0:T(8,128)(2,1)} async-done(((bf16[16,2,128,512]{3,2,1,0:T(8,128)(2,1)}), bf16[16,2,128,512]{3,2,1,0:T(8,128)(2,1)}, u32[]{:S(2)}, u32[]{:S(2)}) %all-to-all-start) | async-done | bytes 4194336 | tf_op jit(solution)/shard_map/all_to_all | solution.py:84
  88.1 5.0 gather_fusion.3
  93.1 4.7 broadcast_select_fusion.1
  97.8 5.2 all-to-all-start.1
  105.7 33.8 %psum.15 = f32[128]{0:T(128)S(1)} all-reduce(f32[128]{0:T(128)S(1)} %multiply_reduce_fusion.1), channel_id=1, replica_groups=mesh['grp'=4,'kv_0'=4,'kv_1'=4,'tp'=2] {'kv_0','kv_1'}, use_global_device_ids=true, to_apply=%region_2.0 | all-reduce | flops 128 | bytes 1024 | tf_op jit(solution)/shard_map/psum | solution.py:175
  139.7 61.2 %all-reduce.2.cloned.1.call-done = f32[128,2048]{1,0:T(8,128)} async-done(((f32[128,2048]{1,0:T(8,128)}), f32[128,2048]{1,0:T(8,128)}) %all-reduce.2.cloned.1.call-update) | async-done | bytes 1048592 | tf_op jit(solution)/shard_map/psum | solution.py:175
  205.5 5.0 gather_fusion.4
  210.6 2.8 broadcast_select_fusion
  213.4 3.0 pad_maximum_fusion
  216.4 4.6 copy.192
  221.0 4.7 copy.187
  225.8 4.6 fusion.80
  231.8 6.9 %fusion.17 = f32[24,4,4,128]{3,2,1,0:T(4,128)S(1)} fusion(bf16[24,128,4,128]{1,3,2,0:T(8,128)(2,1)} %bitcast.217, f32[24,4,4,128]{3,2,1,0:T(4,128)S(1)} %get-tuple-element.48, f32[24,4,4]{2,1,0:T(4,128)S(1)} %broadcast_select_fusion.3, pred[24,128]{1,0:T(8,128)(4,1)S(1)} %iota_compare_fusion), kind=kOutput, calls=%fused_computation.53 | convolution fusion | flops 75595776 | bytes 3543552 | tf_op jit(solution)/shard_map/ikgt,itkd->ikgd/dot_general | solution.py:134
  241.4 9.3 %all_gather.29 = f32[4,128,16]{1,2,0:T(8,128)S(1)} all-gather(f32[1,128,16]{1,2,0:T(8,128)S(1)} %bitcast.229), channel_id=1, replica_groups=mesh['grp'=4,'kv_0'=4,'kv_1'=4,'tp'=2] {'kv_0'}, dimensions={0}, use_global_device_ids=true | all-gather | bytes 40960 | tf_op jit(solution)/shard_map/all_gather | solution.py:22
  251.4 38.9 %all-gather.5.cloned.1.call-done = f32[4,128,16,128]{3,2,1,0:T(8,128)} async-done(((f32[1,128,16,128]{3,2,1,0:T(8,128)}), f32[4,128,16,128]{3,2,1,0:T(8,128)}) %all-gather.5.cloned.1.call-update) | async-done | bytes 4194320 | tf_op jit(solution)/shard_map/all_gather | solution.py:22
  290.2 4.8 fusion.3
  297.2 9.0 %all-gather = f32[512,16]{0,1:T(8,128)S(1)} all-gather(f32[128,16]{0,1:T(8,128)S(1)} %convolution_add_fusion.1), channel_id=2, replica_groups=mesh['grp'=4,'kv_0'=4,'kv_1'=4,'tp'=2] {'kv_0'}, dimensions={0}, use_global_device_ids=true | all-gather | bytes 40960 | tf_op jit(solution)/shard_map/all_gather | solution.py:22
  306.2 10.8 %all_gather.34 = f32[4,128,16]{1,2,0:T(8,128)S(1)} all-gather(f32[1,128,16]{1,2,0:T(8,128)S(1)} %get-tuple-element.22), channel_id=1, replica_groups=mesh['grp'=4,'kv_0'=4,'kv_1'=4,'tp'=2] {'kv_1'}, dimensions={0}, use_global_device_ids=true | all-gather | bytes 40960 | tf_op jit(solution)/shard_map/all_gather | solution.py:22
  317.0 10.6 %all_gather.31 = f32[4,128,16]{1,2,0:T(8,128)S(1)} all-gather(f32[1,128,16]{1,2,0:T(8,128)S(1)} %get-tuple-element.23), channel_id=1, replica_groups=mesh['grp'=4,'kv_0'=4,'kv_1'=4,'tp'=2] {'kv_1'}, dimensions={0}, use_global_device_ids=true | all-gather | bytes 40960 | tf_op jit(solution)/shard_map/all_gather | solution.py:22
  327.7 16.7 %all-gather.7.cloned.1.call-done = f32[4,128,16,128]{3,2,1,0:T(8,128)} async-done(((f32[1,128,16,128]{3,2,1,0:T(8,128)}), f32[4,128,16,128]{3,2,1,0:T(8,128)}) %all-gather.7.cloned.1.call-update) | async-done | bytes 4194320 | tf_op jit(solution)/shard_map/all_gather | solution.py:22
  344.3 3.9 fusion.78
  358.3 114.5 %all-gather.9.cloned.1.call-done = bf16[32,128,4096]{2,1,0:T(8,128)(2,1)} async-done(((bf16[1,128,4096]{2,1,0:T(8,128)(2,1)}), bf16[32,128,4096]{2,1,0:T(8,128)(2,1)}) %all-gather.9.cloned.1.call-update) | async-done | bytes 33554448 | tf_op jit(solution)/shard_map/all_gather | solution.py:206
  472.8 11.4 %reduce_sum.100 = bf16[128,4096]{1,0:T(8,128)(2,1)S(1)} reduce(bf16[32,128,4096]{2,1,0:T(8,128)(2,1)} %all-gather.9.cloned.1.call-done, bf16[]{:T(256)} %constant.131.clone.1), dimensions={0}, to_apply=%region_13.15 | reduce | flops 16252928 | bytes 34603008 | tf_op jit(solution)/shard_map/reduce_sum | solution.py:205
  485.5 3.3 convolution_multiply_fusion.1
  488.7 6.1 %convolution_convert_fusion = bf16[128,4096]{1,0:T(8,128)(2,1)S(1)} fusion(bf16[448,4096]{1,0:T(8,128)(2,1)} %param.26, bf16[4096,448]{0,1:T(8,128)(2,1)} %param.25, f32[4096]{0:T(1024)S(1)} %copy-done.6, bf16[128,4096]{0,1:T(8,128)(2,1)S(1)} %copy.225, f32[128,448]{0,1:T(8,128)S(1)} %convolution_multiply_fusion.1, f32[128]{0:T(128)S(1)} %add_rsqrt_fusion), kind=kOutput, calls=%fused_computation.7 | convolution fusion | flops 942022656 | bytes 9683456 | tf_op jit(solution)/shard_map/dot_general | solution.py:216
  496.0 5.3 all-to-all-start.2
  501.3 4.7 fusion.92
  506.1 12.1 %all-to-all-done.2 = bf16[32,4,4096]{2,1,0:T(4,128)(2,1)} async-done(((bf16[32,4,4096]{2,1,0:T(4,128)(2,1)}), bf16[32,4,4096]{2,1,0:T(4,128)(2,1)}, u32[]{:S(2)}, u32[]{:S(2)}) %all-to-all-start.2) | async-done | bytes 1048608 | tf_op jit(solution)/shard_map/all_to_all | solution.py:36
  521.9 3.2 add_convert_fusion
  (123 shorter events, 36.8 us)
Async XLA Ops:
  7.2 95.8 %copy-start = (bf16[256,2048]{1,0:T(8,128)(2,1)S(1)}, bf16[256,2048]{1,0:T(8,128)(2,1)}, u32[]{:S(2)}) copy-start(bf16[256,2048]{1,0:T(8,128)(2,1)} %param.22) | copy-start | bytes 3145732
  20.1 68.0 %all-to-all-start = ((bf16[16,2,128,512]{3,2,1,0:T(8,128)(2,1)}), bf16[16,2,128,512]{3,2,1,0:T(8,128)(2,1)}, u32[]{:S(2)}, u32[]{:S(2)}) async-start(bf16[16,2,128,512]{3,2,1,0:T(8,128)(2,1)} %broadcast_select_fusion.2), calls=%async_computation | async-start | bytes 8388608 | tf_op jit(solution)/shard_map/all_to_all | solution.py:84
  97.8 5.3 copy-start.5
  97.8 5.3 copy-start.7
  97.8 6.7 %copy-start.8 = (s32[1,16]{1,0:T(1,128)S(1)}, s32[1,16]{1,0:T(1,128)}, u32[]{:S(2)}) copy-start(s32[1,16]{1,0:T(1,128)} %param.33) | copy-start | bytes 196
  97.8 6.7 %copy-start.9 = (s32[1,8]{1,0:T(1,128)S(1)}, s32[1,8]{1,0:T(1,128)}, u32[]{:S(2)}) copy-start(s32[1,8]{1,0:T(1,128)} %param.29) | copy-start | bytes 100
  97.8 7.1 %copy-start.4 = (bf16[128,2,512]{2,1,0:T(2,128)(2,1)S(1)}, bf16[128,2,512]{2,1,0:T(2,128)(2,1)}, u32[]{:S(2)}) copy-start(bf16[128,2,512]{2,1,0:T(2,128)(2,1)} %param.35) | copy-start | bytes 786436
  97.8 107.8 %all-to-all-start.1 = ((bf16[16,2,128,512]{3,2,1,0:T(8,128)(2,1)}), bf16[16,2,128,512]{3,2,1,0:T(8,128)(2,1)}, u32[]{:S(2)}, u32[]{:S(2)}) async-start(bf16[16,2,128,512]{3,2,1,0:T(8,128)(2,1)} %broadcast_select_fusion.1), calls=%async_computation.1 | async-start | bytes 8388608 | tf_op jit(solution)/shard_map/all_to_all | solution.py:100
  103.0 2.3 copy-start.10
  103.0 2.3 copy-start.11
  103.0 98.0 %all-reduce.2.cloned.1.call-start = ((), (), s32[]{:S(2)}) async-start(), calls=%async_computation.3 | async-start | bytes 2097152 | tf_op jit(solution)/shard_map/psum | solution.py:175
  104.4 185.8 %all-gather.5.cloned.1.call-start = ((), (), s32[]{:S(2)}) async-start(), calls=%async_computation.4 | async-start | bytes 5242880 | tf_op jit(solution)/shard_map/all_gather | solution.py:22
  210.6 2.9 copy-start.2
  241.3 103.0 %all-gather.7.cloned.1.call-start = ((), (), s32[]{:S(2)}) async-start(), calls=%async_computation.5 | async-start | bytes 5242880 | tf_op jit(solution)/shard_map/all_gather | solution.py:22
  250.8 44.4 %copy-start.3 = (bf16[16,8,4096]{2,1,0:T(8,128)(2,1)S(1)}, bf16[16,8,4096]{2,1,0:T(8,128)(2,1)}, u32[]{:S(2)}) copy-start(bf16[16,8,4096]{2,1,0:T(8,128)(2,1)} %param.23) | copy-start | bytes 3145732
  295.1 177.8 %all-gather.9.cloned.1.call-start = ((), (), s32[]{:S(2)}) async-start(), calls=%async_computation.6 | async-start | bytes 34603008 | tf_op jit(solution)/shard_map/all_gather | solution.py:206
  358.3 127.2 %copy-start.6 = (f32[4096]{0:T(1024)S(1)}, f32[4096]{0:T(1024)}, u32[]{:S(2)}) copy-start(f32[4096]{0:T(1024)} %param.21) | copy-start | bytes 49156
  496.0 22.2 %all-to-all-start.2 = ((bf16[32,4,4096]{2,1,0:T(4,128)(2,1)}), bf16[32,4,4096]{2,1,0:T(4,128)(2,1)}, u32[]{:S(2)}, u32[]{:S(2)}) async-start(bf16[32,4,4096]{2,1,0:T(4,128)(2,1)} %reshape.681), calls=%async_computation.2 | async-start | bytes 2097152 | tf_op jit(solution)/shard_map/all_to_all | solution.py:36
  519.9 7.4 %copy-start.1 = (bf16[256,2048]{1,0:T(8,128)(2,1)S(1)}, bf16[256,2048]{1,0:T(8,128)(2,1)}, u32[]{:S(2)}) copy-start(bf16[256,2048]{1,0:T(8,128)(2,1)} %param.22) | copy-start | bytes 3145732
Sparse Core Ops, SparseCore 0:
  107.0 93.8 all-reduce.1
  241.4 48.7 all-gather.4
  295.2 49.0 all-gather.6
  358.4 114.3 all-gather.8
